TPU v7x, 32 devices: a whole 2x2x4 slice. The times are simulated.
32 devices in a mesh: dp: 8 (over z, core), tensor: 4 (over y, x).
Axes of the slice: x: 2, y: 2, z: 4, core: 2. Of those that a mesh axis runs over, the one named last changes fastest.
Arguments:
- block_input: bfloat16 [8192, 2048], P(('dp', 'tensor')), may hold values from -6 to 6
- attn_gain: float32 [2048], replicated, may hold values from 0.5 to 1.5
- w_query: bfloat16 [2048, 2048], P('dp', 'tensor'), may hold values from -6 to 6
- w_key: bfloat16 [2048, 512], P('dp', 'tensor'), may hold values from -0.125 to 0.125
- w_value: bfloat16 [2048, 512], P('dp', 'tensor'), may hold values from -0.125 to 0.125
- w_out: bfloat16 [2048, 2048], P('dp', 'tensor'), may hold values from -0.5 to 0.5
- mlp_gain: float32 [2048], replicated, may hold values from 0.5 to 1.5
- w_gate: bfloat16 [2048, 8192], P('dp', 'tensor'), may hold values from -0.125 to 0.125
- w_up: bfloat16 [2048, 8192], P('dp', 'tensor'), may hold values from -0.125 to 0.125
- w_down: bfloat16 [2048, 8192], P('dp', 'tensor'), may hold values from -0.0625 to 0.0625
- doc_ids: int32 [8192], P('dp'), may hold values from -1 to 3, as said below
- cotangent: bfloat16 [8192, 2048], P(('dp', 'tensor')), may hold values from -6 to 6
Outputs:
- block_output: bfloat16 [8192, 2048], P(('dp', 'tensor'))
- input_grad: bfloat16 [8192, 2048], P(('dp', 'tensor'))
- grad_query: float32 [2048, 2048], P('dp', 'tensor')
- grad_key: float32 [2048, 512], P('dp', 'tensor')
- grad_value: float32 [2048, 512], P('dp', 'tensor')
- grad_out: float32 [2048, 2048], P('dp', 'tensor')
- grad_gate: float32 [2048, 8192], P('dp', 'tensor')
- grad_up: float32 [2048, 8192], P('dp', 'tensor')
- grad_down: float32 [2048, 8192], P('dp', 'tensor')
- grad_attn_gain: float32 [2048], replicated
- grad_mlp_gain: float32 [2048], replicated
Inputs may be any that keep to these rules, and one draw needn't show every extreme that they name: `doc_ids`: within each aligned block of 512 positions the ids of live positions never fall; -1 marks padding, which only ends a block; a block whose first position is -1 is padding throughout; every block ends with padding; a live block has at least 256 live positions; some index of dp has all its 2 blocks live, others may have fewer.
All inputs are finite; a program needn't handle non-finite values.
Results may differ from a plain program's by a relative error of at most 0.014.
The roundings to bfloat16 on the way count: a program that leaves them out, or rounds other values in their place, can miss the bound.
Values may be sent and summed in bfloat16 or wider, within the bound.
A program may use at most 256 MiB of HBM per device.

v0:
```python
import jax
import jax.numpy as jnp
from jax import lax
from jax.sharding import PartitionSpec as P

HD = 64
SEQ = 512
EPSILON = 1e-05
ROPE_BASE = 500000.0
NEG_LARGE = -1e30


def rotary_tables(length, head_dim):
    half_dim = head_dim // 2
    frequency = ROPE_BASE ** (-(jnp.arange(half_dim, dtype=jnp.float32) * (2.0 / head_dim)))
    angles = jnp.arange(length, dtype=jnp.float32)[:, None] * frequency[None, :]
    angles = jnp.concatenate([angles, angles], axis=1)
    return (jnp.cos(angles), jnp.sin(angles))


def rotate_half(tensor_rows):
    half_dim = tensor_rows.shape[-1] // 2
    return jnp.concatenate([-tensor_rows[..., half_dim:], tensor_rows[..., :half_dim]], axis=-1)


def rotate_back(tensor_rows):
    half_dim = tensor_rows.shape[-1] // 2
    return jnp.concatenate([tensor_rows[..., half_dim:], -tensor_rows[..., :half_dim]], axis=-1)


def apply_rotary(tensor_rows, cosine_table, sine_table):
    return (
        tensor_rows * cosine_table[:, None, :] + rotate_half(tensor_rows) * sine_table[:, None, :]
    )


def undo_rotary(tensor_rows, cosine_table, sine_table):
    return tensor_rows * cosine_table[:, None, :] + rotate_back(
        tensor_rows * sine_table[:, None, :]
    )


def norm_scale(tensor_rows):
    return lax.rsqrt(jnp.mean(tensor_rows * tensor_rows, axis=1, keepdims=True) + EPSILON)


def norm_back(grad_normed, tensor_rows, row_scale, gain_row):
    weighted = grad_normed * gain_row[None, :]
    inner_mean = jnp.mean(weighted * tensor_rows, axis=1, keepdims=True)
    return row_scale * weighted - tensor_rows * (row_scale * row_scale * row_scale) * inner_mean


def slot_mask(doc_rows):
    positions = jnp.arange(doc_rows.shape[0])
    earlier = positions[None, :] <= positions[:, None]
    same_doc = (doc_rows[:, None] == doc_rows[None, :]) & (doc_rows[:, None] >= 0)
    return same_doc & earlier | (positions[None, :] == positions[:, None])


def contract_rows(left_side, right_side):
    return lax.dot_general(
        left_side, right_side, (((0,), (0,)), ((), ())), preferred_element_type=jnp.float32
    )


def contract_cols(left_side, right_side):
    return lax.dot_general(
        left_side, right_side, (((1,), (1,)), ((), ())), preferred_element_type=jnp.float32
    )


def slot_scores(query_rows, key_rows, allowed):
    seq_len, head_count, head_dim = query_rows.shape
    groups = key_rows.shape[1]
    grouped = query_rows.reshape(seq_len, groups, head_count // groups, head_dim)
    scores = jnp.einsum(
        "sgjd,tgd->gjst", grouped, key_rows, preferred_element_type=jnp.float32
    ) * head_dim ** (-0.5)
    return (grouped, jnp.where(allowed[None, None], scores, NEG_LARGE))


def attend(packed):
    query_rows, key_rows, value_rows, doc_rows = packed
    seq_len, head_count, head_dim = query_rows.shape
    allowed = slot_mask(doc_rows)
    live_rows = (doc_rows >= 0).astype(jnp.float32)
    grouped, scores = slot_scores(query_rows, key_rows, allowed)
    row_max = jnp.max(scores, axis=-1, keepdims=True)
    weights = jnp.exp(scores - row_max)
    row_total = jnp.sum(weights, axis=-1, keepdims=True)
    prob_bf = (weights / row_total).astype(jnp.bfloat16)
    mixed_rows = jnp.einsum(
        "gjst,tgd->sgjd", prob_bf, value_rows, preferred_element_type=jnp.float32
    )
    mixed_rows = mixed_rows.reshape(seq_len, head_count * head_dim) * live_rows[:, None]
    return (mixed_rows.astype(jnp.bfloat16), row_max + jnp.log(row_total))


def attend_back(packed):
    query_rows, key_rows, value_rows, doc_rows, log_total, grad_mixed = packed
    seq_len, head_count, head_dim = query_rows.shape
    groups = key_rows.shape[1]
    allowed = slot_mask(doc_rows)
    grouped, scores = slot_scores(query_rows, key_rows, allowed)
    prob_full = jnp.where(allowed[None, None], jnp.exp(scores - log_total), 0.0)
    grad_rows = grad_mixed.reshape(seq_len, groups, head_count // groups, head_dim)
    grad_prob = jnp.einsum(
        "sgjd,tgd->gjst", grad_rows, value_rows, preferred_element_type=jnp.float32
    )
    row_delta = jnp.sum(prob_full * grad_prob, axis=-1, keepdims=True)
    grad_scores = (prob_full * (grad_prob - row_delta)).astype(jnp.bfloat16)
    grad_values = jnp.einsum(
        "gjst,sgjd->tgd",
        prob_full.astype(jnp.bfloat16),
        grad_rows,
        preferred_element_type=jnp.float32,
    )
    grad_queries = jnp.einsum(
        "gjst,tgd->sgjd", grad_scores, key_rows, preferred_element_type=jnp.float32
    ) * head_dim ** (-0.5)
    grad_keys = jnp.einsum(
        "gjst,sgjd->tgd", grad_scores, grouped, preferred_element_type=jnp.float32
    ) * head_dim ** (-0.5)
    return (grad_queries.reshape(seq_len, head_count, head_dim), grad_keys, grad_values)


def sum_rows(partial, axis):
    return lax.psum_scatter(
        partial.astype(jnp.bfloat16), axis, scatter_dimension=0, tiled=True
    ).astype(jnp.float32)


def per_device(
    block_input,
    attn_gain,
    w_query,
    w_key,
    w_value,
    w_out,
    mlp_gain,
    w_gate,
    w_up,
    w_down,
    doc_ids,
    cotangent,
):
    query_full, key_full, value_full, out_full, gate_full, up_full, down_full = (
        lax.all_gather(w_query, "dp", axis=0, tiled=True),
        lax.all_gather(w_key, "dp", axis=0, tiled=True),
        lax.all_gather(w_value, "dp", axis=0, tiled=True),
        lax.all_gather(w_out, "dp", axis=0, tiled=True),
        lax.all_gather(w_gate, "dp", axis=0, tiled=True),
        lax.all_gather(w_up, "dp", axis=0, tiled=True),
        lax.all_gather(w_down, "dp", axis=0, tiled=True),
    )
    total_rows = doc_ids.shape[0]
    slot_count = total_rows // SEQ
    local_heads = query_full.shape[1] // HD
    local_groups = key_full.shape[1] // HD
    cosine_table, sine_table = rotary_tables(SEQ, HD)
    live_all = (doc_ids >= 0).astype(jnp.float32)
    input_own = block_input.astype(jnp.float32)
    scale_one = norm_scale(input_own)
    normed_one = lax.all_gather(
        (input_own * scale_one * attn_gain[None, :]).astype(jnp.bfloat16),
        "tensor",
        axis=0,
        tiled=True,
    )
    query_pre = jnp.dot(normed_one, query_full, preferred_element_type=jnp.float32).reshape(
        slot_count, SEQ, local_heads, HD
    )
    key_pre = jnp.dot(normed_one, key_full, preferred_element_type=jnp.float32).reshape(
        slot_count, SEQ, local_groups, HD
    )
    query_rows = apply_rotary(query_pre, cosine_table, sine_table).astype(jnp.bfloat16)
    key_rows = apply_rotary(key_pre, cosine_table, sine_table).astype(jnp.bfloat16)
    value_rows = (
        jnp.dot(normed_one, value_full, preferred_element_type=jnp.float32)
        .astype(jnp.bfloat16)
        .reshape(slot_count, SEQ, local_groups, HD)
    )
    doc_slots = doc_ids.reshape(slot_count, SEQ)
    mixed_slots, log_total = lax.map(attend, (query_rows, key_rows, value_rows, doc_slots))
    mixed_all = mixed_slots.reshape(total_rows, local_heads * HD)
    residual_own = input_own + sum_rows(contract_cols(mixed_all, out_full), "tensor")
    scale_two_own = norm_scale(residual_own)
    normed_two = lax.all_gather(
        (residual_own * scale_two_own * mlp_gain[None, :]).astype(jnp.bfloat16),
        "tensor",
        axis=0,
        tiled=True,
    )
    gate_pre = jnp.dot(normed_two, gate_full, preferred_element_type=jnp.float32)
    up_pre = jnp.dot(normed_two, up_full, preferred_element_type=jnp.float32)
    sigmoid_gate = jax.nn.sigmoid(gate_pre)
    silu_gate = gate_pre * sigmoid_gate
    hidden = (silu_gate * up_pre).astype(jnp.bfloat16)
    block_output = (residual_own + sum_rows(contract_cols(hidden, down_full), "tensor")).astype(
        jnp.bfloat16
    )
    grad_full = lax.all_gather(cotangent, "tensor", axis=0, tiled=True)
    grad_hidden = jnp.dot(grad_full, down_full, preferred_element_type=jnp.float32)
    grad_down = contract_rows(grad_full, hidden)
    grad_gate_pre = (
        grad_hidden * up_pre * sigmoid_gate * (1.0 + gate_pre * (1.0 - sigmoid_gate))
    ).astype(jnp.bfloat16)
    grad_up_pre = (grad_hidden * silu_gate).astype(jnp.bfloat16)
    grad_gate = contract_rows(normed_two, grad_gate_pre)
    grad_up = contract_rows(normed_two, grad_up_pre)
    grad_normed_own = sum_rows(
        contract_cols(grad_gate_pre, gate_full) + contract_cols(grad_up_pre, up_full), "tensor"
    )
    grad_mlp_gain = jnp.sum(grad_normed_own * residual_own * scale_two_own, axis=0)
    grad_residual_own = cotangent.astype(jnp.float32) + norm_back(
        grad_normed_own, residual_own, scale_two_own, mlp_gain
    )
    grad_residual_bf = lax.all_gather(
        grad_residual_own.astype(jnp.bfloat16), "tensor", axis=0, tiled=True
    )
    grad_out = contract_rows(grad_residual_bf, mixed_all)
    grad_mixed = (
        jnp.dot(grad_residual_bf, out_full, preferred_element_type=jnp.float32) * live_all[:, None]
    ).astype(jnp.bfloat16)
    grad_mixed_slots = grad_mixed.reshape(slot_count, SEQ, local_heads * HD)
    grad_queries, grad_keys, grad_values = lax.map(
        attend_back, (query_rows, key_rows, value_rows, doc_slots, log_total, grad_mixed_slots)
    )
    grad_query_rows = (
        undo_rotary(grad_queries, cosine_table, sine_table)
        .astype(jnp.bfloat16)
        .reshape(total_rows, local_heads * HD)
    )
    grad_key_rows = (
        undo_rotary(grad_keys, cosine_table, sine_table)
        .astype(jnp.bfloat16)
        .reshape(total_rows, local_groups * HD)
    )
    grad_value_rows = grad_values.astype(jnp.bfloat16).reshape(total_rows, local_groups * HD)
    grad_query = contract_rows(normed_one, grad_query_rows)
    grad_key = contract_rows(normed_one, grad_key_rows)
    grad_value = contract_rows(normed_one, grad_value_rows)
    grad_normed_one = sum_rows(
        contract_cols(grad_query_rows, query_full)
        + contract_cols(grad_key_rows, key_full)
        + contract_cols(grad_value_rows, value_full),
        "tensor",
    )
    grad_attn_gain = jnp.sum(grad_normed_one * input_own * scale_one, axis=0)
    input_grad = (
        grad_residual_own + norm_back(grad_normed_one, input_own, scale_one, attn_gain)
    ).astype(jnp.bfloat16)
    summed = (
        sum_rows(grad_query, "dp"),
        sum_rows(grad_key, "dp"),
        sum_rows(grad_value, "dp"),
        sum_rows(grad_out, "dp"),
        sum_rows(grad_gate, "dp"),
        sum_rows(grad_up, "dp"),
        sum_rows(grad_down, "dp"),
    )
    gains = lax.psum((grad_attn_gain, grad_mlp_gain), ("dp", "tensor"))
    return (
        block_output,
        input_grad,
        summed[0],
        summed[1],
        summed[2],
        summed[3],
        summed[4],
        summed[5],
        summed[6],
        gains[0],
        gains[1],
    )


def solution(mesh):
    in_specs = (
        P(("dp", "tensor"), None),
        P(),
        P("dp", "tensor"),
        P("dp", "tensor"),
        P("dp", "tensor"),
        P("dp", "tensor"),
        P(),
        P("dp", "tensor"),
        P("dp", "tensor"),
        P("dp", "tensor"),
        P("dp"),
        P(("dp", "tensor"), None),
    )
    out_specs = (
        P(("dp", "tensor"), None),
        P(("dp", "tensor"), None),
        P("dp", "tensor"),
        P("dp", "tensor"),
        P("dp", "tensor"),
        P("dp", "tensor"),
        P("dp", "tensor"),
        P("dp", "tensor"),
        P("dp", "tensor"),
        P(),
        P(),
    )
    return jax.shard_map(
        per_device, mesh=mesh, in_specs=in_specs, out_specs=out_specs, check_vma=False
    )
```

profile of v0, /device:TPU:0, one launch (start us, length us, event | category | flops | bytes accessed | tf_op | source)
XLA Modules:
  0.0 1358.1 jit_solution(2568812626579666158)
XLA Ops:
  14.4 18.8 %all_gather.35 = bf16[2048,128]{1,0:T(8,128)(2,1)S(1)} all-gather(bf16[256,128]{1,0:T(8,128)(2,1)S(1)} %copy-done.32), channel_id=1, replica_groups=mesh['dp'=8,'tensor'=4] {'dp'}, dimensions={0}, use_global_device_ids=true | all-gather | bytes 589824 | tf_op jit(solution)/shard_map/all_gather | solution.py:149
  33.2 18.2 %all_gather.34 = bf16[2048,128]{1,0:T(8,128)(2,1)} all-gather(bf16[256,128]{1,0:T(8,128)(2,1)S(1)} %copy-done.33), channel_id=1, replica_groups=mesh['dp'=8,'tensor'=4] {'dp'}, dimensions={0}, use_global_device_ids=true | all-gather | bytes 589824 | tf_op jit(solution)/shard_map/all_gather | solution.py:150
  51.5 50.4 %all-gather.10.cloned.1.call-done = bf16[1024,2048]{1,0:T(8,128)(2,1)} async-done(((bf16[256,2048]{1,0:T(8,128)(2,1)}), bf16[1024,2048]{1,0:T(8,128)(2,1)}) %all-gather.10.cloned.1.call-update) | async-done | bytes 4194320 | tf_op jit(solution)/shard_map/all_gather | solution.py:164
  121.3 14.8 %while.26 = (s32[]{:T(128)}, bf16[2,512,512]{2,1,0:T(8,128)(2,1)}, f32[2,2,4,512,1]{3,2,1,4,0:T(4,128)S(1)}, bf16[2,512,2,64]{1,3,2,0:T(8,128)(2,1)S(1)}, s32[2,...) while((s32[]{:T(128)}, bf16[2,512,512]{2,1,0:T(8,128)(2,1)}, ...), condition=%wide.region_4.5_spmd, body=%wide.region_1.4_spmd.sunk | while | flops 564130816 | bytes 32913000 | solution.py:184
  143.3 52.2 %reduce-scatter.12.cloned.1.call-done = bf16[256,2048]{1,0:T(8,128)(2,1)} async-done(((bf16[1024,2048]{1,0:T(8,128)(2,1)}), bf16[256,2048]{1,0:T(8,128)(2,1)}) %reduce-scatter.12.cloned.1.call-update) | async-done | bytes 1048592 | tf_op jit(solution)/shard_map/reduce_scatter | solution.py:128
  202.0 76.9 %all-gather.18.cloned.1.call-done = bf16[2048,2048]{1,0:T(8,128)(2,1)} async-done(((bf16[256,2048]{1,0:T(8,128)(2,1)}), bf16[2048,2048]{1,0:T(8,128)(2,1)}) %all-gather.18.cloned.1.call-update) | async-done | bytes 8388624 | tf_op jit(solution)/shard_map/all_gather | solution.py:152
  279.0 53.4 %all-gather.16.cloned.1.call-done = bf16[1024,2048]{1,0:T(8,128)(2,1)} async-done(((bf16[256,2048]{1,0:T(8,128)(2,1)}), bf16[1024,2048]{1,0:T(8,128)(2,1)}) %all-gather.16.cloned.1.call-update) | async-done | bytes 4194320 | tf_op jit(solution)/shard_map/all_gather | solution.py:188
  332.3 14.6 %fusion.75 = f32[1024,2048]{1,0:T(8,128)} fusion(bf16[1024,2048]{1,0:T(8,128)(2,1)} %all-gather.16.cloned.1.call-done, bf16[2048,2048]{1,0:T(8,128)(2,1)} %all-gather.18.cloned.1.call-done), kind=kOutput, calls=%fused_computation.143 | convolution fusion | flops 8589934592 | bytes 20971520 | tf_op jit(solution)/shard_map/dot_general | solution.py:194
  347.0 69.0 %all-gather.20.cloned.1.call-done = bf16[2048,2048]{1,0:T(8,128)(2,1)} async-done(((bf16[256,2048]{1,0:T(8,128)(2,1)}), bf16[2048,2048]{1,0:T(8,128)(2,1)}) %all-gather.20.cloned.1.call-update) | async-done | bytes 8388624 | tf_op jit(solution)/shard_map/all_gather | solution.py:153
  416.0 14.5 %fusion.76 = f32[1024,2048]{1,0:T(8,128)} fusion(bf16[1024,2048]{1,0:T(8,128)(2,1)} %all-gather.16.cloned.1.call-done, bf16[2048,2048]{1,0:T(8,128)(2,1)} %all-gather.20.cloned.1.call-done), kind=kOutput, calls=%fused_computation.144 | convolution fusion | flops 8589934592 | bytes 20971520 | tf_op jit(solution)/shard_map/dot_general | solution.py:195
  430.5 38.5 %all-gather.24.cloned.1.call-done = bf16[1024,2048]{1,0:T(8,128)(2,1)} async-done(((bf16[256,2048]{1,0:T(8,128)(2,1)}), bf16[1024,2048]{1,0:T(8,128)(2,1)}) %all-gather.24.cloned.1.call-update) | async-done | bytes 4194320 | tf_op jit(solution)/shard_map/all_gather | solution.py:202
  468.9 83.7 %all-gather.22.cloned.1.call-done = bf16[2048,2048]{1,0:T(8,128)(2,1)} async-done(((bf16[256,2048]{1,0:T(8,128)(2,1)}), bf16[2048,2048]{1,0:T(8,128)(2,1)}) %all-gather.22.cloned.1.call-update) | async-done | bytes 8388624 | tf_op jit(solution)/shard_map/all_gather | solution.py:154
  552.6 21.1 %multiply_convert_fusion.1 = (bf16[1024,2048]{1,0:T(8,128)(2,1)S(1)}, bf16[1024,2048]{1,0:T(8,128)(2,1)}, bf16[1024,2048]{1,0:T(8,128)(2,1)}) fusion(f32[1024,2048]{1,0:T(8,128)} %fusion.75, f32[1024,2048]{1,0:T(8,128)} %fusion.76, bf16[1024,2048]{1,0:T(8,128)(2,1)} %all-gather.24.cloned.1.call-done, bf16[2048,2048]{1,0:T(8,128)(2,1)} %all-gather.22.cloned.1.call-done), kind=kOutput, calls=%fused_computation.64 | convolution fusion | flops 8621391872 | bytes 41943040 | tf_op jit(solution)/shard_map/dot_general | solution.py:203
  573.7 16.6 %fusion.77 = f32[1024,2048]{1,0:T(8,128)} fusion(bf16[1024,2048]{1,0:T(8,128)(2,1)} %get-tuple-element.211, bf16[2048,2048]{1,0:T(8,128)(2,1)} %all-gather.18.cloned.1.call-done), kind=kOutput, calls=%fused_computation.145 | convolution fusion | flops 8589934592 | bytes 20971520 | tf_op jit(solution)/shard_map/dot_general | solution.py:67
  590.4 12.4 add_convert_fusion.1
  602.8 51.2 %reduce-scatter.16.cloned.1.call-done = bf16[256,2048]{1,0:T(8,128)(2,1)} async-done(((bf16[1024,2048]{1,0:T(8,128)(2,1)}), bf16[256,2048]{1,0:T(8,128)(2,1)}) %reduce-scatter.16.cloned.1.call-update) | async-done | bytes 1048592 | tf_op jit(solution)/shard_map/reduce_scatter | solution.py:128
  660.0 52.6 %all-gather.26.cloned.1.call-done = bf16[1024,2048]{1,0:T(8,128)(2,1)} async-done(((bf16[256,2048]{1,0:T(8,128)(2,1)}), bf16[1024,2048]{1,0:T(8,128)(2,1)}) %all-gather.26.cloned.1.call-update) | async-done | bytes 4194320 | tf_op jit(solution)/shard_map/all_gather | solution.py:218
  717.9 105.9 %while.27 = (s32[]{:T(128)}, f32[2,512,8,64]{1,0,3,2:T(2,128)}, f32[2,512,2,64]{1,0,3,2:T(2,128)}, bf16[2,512,2,64]{1,3,2,0:T(8,128)(2,1)}, bf16[2,512,2,64]{1,3...) while((s32[]{:T(128)}, f32[2,512,8,64]{1,0,3,2:T(2,128)}, ...), condition=%wide.region_12.13_spmd, body=%wide.region_10.12_spmd.sunk | while | flops 1365045760 | bytes 147417520 | solution.py:226
  738.6 19.7 %dynamic_update_slice.30 = f32[2,512,8,64]{1,0,3,2:T(2,128)} dynamic-update-slice(f32[2,512,8,64]{1,0,3,2:T(2,128)} %get-tuple-element.382, f32[1,512,8,64]{1,0,3,2:T(1,128)S(1)} %copy.94, s32[]{:T(128)} %get-tuple-element.381, s32[]{:T(128)} %constant.45.clone.1..sunk, s32[]{:T(128)} %constant.45.clone.1..sunk, s32[]{:T(128)} %constant.45.clone.1..sunk) | dynamic-update-slice | bytes 2097156 | tf_op jit(solution)/shard_map/while/body/jit(dynamic_update_index_in_dim)/dynamic_update_slice | solution.py:226
  791.4 19.7 %dynamic_update_slice.30 = f32[2,512,8,64]{1,0,3,2:T(2,128)} dynamic-update-slice(f32[2,512,8,64]{1,0,3,2:T(2,128)} %get-tuple-element.382, f32[1,512,8,64]{1,0,3,2:T(1,128)S(1)} %copy.94, s32[]{:T(128)} %get-tuple-element.381, s32[]{:T(128)} %constant.45.clone.1..sunk, s32[]{:T(128)} %constant.45.clone.1..sunk, s32[]{:T(128)} %constant.45.clone.1..sunk) | dynamic-update-slice | bytes 2097156 | tf_op jit(solution)/shard_map/while/body/jit(dynamic_update_index_in_dim)/dynamic_update_slice | solution.py:226
  834.1 14.1 %convolution_convert_fusion.1 = bf16[2048,2048]{1,0:T(8,128)(2,1)} fusion(bf16[1024,2048]{1,0:T(8,128)(2,1)} %all-gather.16.cloned.1.call-done, bf16[1024,2048]{1,0:T(8,128)(2,1)} %get-tuple-element.211), kind=kOutput, calls=%fused_computation.70 | convolution fusion | flops 8594128896 | bytes 16777216 | tf_op jit(solution)/shard_map/dot_general | solution.py:61
  848.3 14.2 %convolution_convert_fusion = bf16[2048,2048]{1,0:T(8,128)(2,1)} fusion(bf16[1024,2048]{1,0:T(8,128)(2,1)} %all-gather.16.cloned.1.call-done, bf16[1024,2048]{1,0:T(8,128)(2,1)} %copy-done.48), kind=kOutput, calls=%fused_computation.69 | convolution fusion | flops 8594128896 | bytes 16777216 | tf_op jit(solution)/shard_map/dot_general | solution.py:61
  863.0 14.0 %convert_bitcast_fusion = bf16[2048,2048]{0,1:T(8,128)(2,1)} fusion(bf16[1024,2048]{1,0:T(8,128)(2,1)} %get-tuple-element.212, bf16[1024,2048]{1,0:T(8,128)(2,1)} %all-gather.24.cloned.1.call-done), kind=kOutput, calls=%fused_computation.61 | convolution fusion | flops 8594128896 | bytes 16777216 | tf_op jit(solution)/shard_map/dot_general | solution.py:61
  898.9 14.3 %convolution_convert_fusion.2 = bf16[1024,2048]{1,0:T(8,128)(2,1)} fusion(bf16[1024,2048]{1,0:T(8,128)(2,1)} %get-tuple-element.212, bf16[2048,2048]{1,0:T(8,128)(2,1)} %all-gather.22.cloned.1.call-done), kind=kOutput, calls=%fused_computation.77 | convolution fusion | flops 8592031744 | bytes 16777216 | tf_op jit(solution)/shard_map/dot_general | solution.py:67
  916.3 66.6 %reduce-scatter.28.cloned.1.call-done = bf16[256,2048]{1,0:T(8,128)(2,1)} async-done(((bf16[2048,2048]{1,0:T(8,128)(2,1)}), bf16[256,2048]{1,0:T(8,128)(2,1)}) %reduce-scatter.28.cloned.1.call-update) | async-done | bytes 1048592 | tf_op jit(solution)/shard_map/reduce_scatter | solution.py:128
  985.7 87.4 %reduce-scatter.30.cloned.1.call-done = bf16[256,2048]{1,0:T(8,128)(2,1)} async-done(((bf16[2048,2048]{1,0:T(8,128)(2,1)}), bf16[256,2048]{1,0:T(8,128)(2,1)}) %reduce-scatter.30.cloned.1.call-update) | async-done | bytes 1048592 | tf_op jit(solution)/shard_map/reduce_scatter | solution.py:128
  1075.9 87.3 %reduce-scatter.32.cloned.1.call-done = bf16[256,2048]{0,1:T(8,128)(2,1)} async-done(((bf16[2048,2048]{0,1:T(8,128)(2,1)}), bf16[256,2048]{0,1:T(8,128)(2,1)}) %reduce-scatter.32.cloned.1.call-update) | async-done | bytes 1048592 | tf_op jit(solution)/shard_map/reduce_scatter | solution.py:128
  1165.8 34.1 %reduce-scatter.26.cloned.1.call-done = bf16[256,512]{1,0:T(8,128)(2,1)} async-done(((bf16[2048,512]{1,0:T(8,128)(2,1)}), bf16[256,512]{1,0:T(8,128)(2,1)}) %reduce-scatter.26.cloned.1.call-update) | async-done | bytes 262160 | tf_op jit(solution)/shard_map/reduce_scatter | solution.py:128
  1201.7 35.0 %reduce-scatter.20.cloned.1.call-done = bf16[256,512]{1,0:T(8,128)(2,1)} async-done(((bf16[2048,512]{1,0:T(8,128)(2,1)}), bf16[256,512]{1,0:T(8,128)(2,1)}) %reduce-scatter.20.cloned.1.call-update) | async-done | bytes 262160 | tf_op jit(solution)/shard_map/reduce_scatter | solution.py:128
  1238.5 52.4 %reduce-scatter.18.cloned.1.call-done = bf16[256,2048]{1,0:T(8,128)(2,1)} async-done(((bf16[1024,2048]{1,0:T(8,128)(2,1)}), bf16[256,2048]{1,0:T(8,128)(2,1)}) %reduce-scatter.18.cloned.1.call-update) | async-done | bytes 1048592 | tf_op jit(solution)/shard_map/reduce_scatter | solution.py:128
  1292.8 39.9 %all-reduce = (f32[2048]{0:T(1024)}, f32[2048]{0:T(1024)}) all-reduce(f32[2048]{0:T(1024)S(1)} %get-tuple-element.166, f32[2048]{0:T(1024)S(1)} %copy-done.34), channel_id=1, replica_groups=mesh['dp'=8,'tensor'=4] {'dp','tensor'}, use_global_device_ids=true, to_apply=%region_23.24 | all-reduce | flops 4096 | bytes 32768 | tf_op jit(solution)/shard_map/psum | solution.py:262
  1332.7 14.0 %reduce-scatter.14.cloned.1.call-done = bf16[256,2048]{1,0:T(8,128)(2,1)} async-done(((bf16[1024,2048]{1,0:T(8,128)(2,1)}), bf16[256,2048]{1,0:T(8,128)(2,1)}) %reduce-scatter.14.cloned.1.call-update) | async-done | bytes 1048592 | tf_op jit(solution)/shard_map/reduce_scatter | solution.py:128
  (275 shorter events, 185.5 us)
Async XLA Ops:
  7.2 44.2 %all-gather.12.cloned.1.call-start = ((), (), s32[]{:S(2)}) async-start(), calls=%async_computation.12 | async-start | bytes 2359296 | tf_op jit(solution)/shard_map/all_gather | solution.py:148
  7.9 93.9 %all-gather.10.cloned.1.call-start = ((), (), s32[]{:S(2)}) async-start(), calls=%async_computation.11 | async-start | bytes 5242880 | tf_op jit(solution)/shard_map/all_gather | solution.py:164
  13.2 123.0 %all-gather.14.cloned.1.call-start = ((), (), s32[]{:S(2)}) async-start(), calls=%async_computation.13 | async-start | bytes 2359296 | tf_op jit(solution)/shard_map/all_gather | solution.py:151
  13.9 181.5 %reduce-scatter.12.cloned.1.call-start = ((), (), s32[]{:S(2)}) async-start(), calls=%async_computation.14 | async-start | bytes 5242880 | tf_op jit(solution)/shard_map/reduce_scatter | solution.py:128
  142.6 136.4 %all-gather.18.cloned.1.call-start = ((), (), s32[]{:S(2)}) async-start(), calls=%async_computation.16 | async-start | bytes 9437184 | tf_op jit(solution)/shard_map/all_gather | solution.py:152
  143.2 189.1 %all-gather.16.cloned.1.call-start = ((), (), s32[]{:S(2)}) async-start(), calls=%async_computation.15 | async-start | bytes 5242880 | tf_op jit(solution)/shard_map/all_gather | solution.py:188
  197.1 459.4 %copy-start.35 = (f32[256]{0:T(256)}, f32[256]{0:T(256)S(1)}, u32[]{:S(2)}) copy-start(f32[256]{0:T(256)S(1)} %get-tuple-element.228) | copy-start | bytes 3076
  197.1 459.4 %copy-start.41 = (f32[256]{0:T(256)}, f32[256]{0:T(256)S(1)}, u32[]{:S(2)}) copy-start(f32[256]{0:T(256)S(1)} %get-tuple-element.227) | copy-start | bytes 3076
  199.8 216.3 %all-gather.20.cloned.1.call-start = ((), (), s32[]{:S(2)}) async-start(), calls=%async_computation.17 | async-start | bytes 9437184 | tf_op jit(solution)/shard_map/all_gather | solution.py:153
  200.5 268.4 %all-gather.24.cloned.1.call-start = ((), (), s32[]{:S(2)}) async-start(), calls=%async_computation.20 | async-start | bytes 5242880 | tf_op jit(solution)/shard_map/all_gather | solution.py:202
  201.3 351.4 %all-gather.22.cloned.1.call-start = ((), (), s32[]{:S(2)}) async-start(), calls=%async_computation.18 | async-start | bytes 9437184 | tf_op jit(solution)/shard_map/all_gather | solution.py:154
  202.0 452.0 %reduce-scatter.16.cloned.1.call-start = ((), (), s32[]{:S(2)}) async-start(), calls=%async_computation.21 | async-start | bytes 5242880 | tf_op jit(solution)/shard_map/reduce_scatter | solution.py:128
  602.8 109.9 %all-gather.26.cloned.1.call-start = ((), (), s32[]{:S(2)}) async-start(), calls=%async_computation.22 | async-start | bytes 5242880 | tf_op jit(solution)/shard_map/all_gather | solution.py:218
  659.9 253.4 %reduce-scatter.22.cloned.1.call-start = ((), (), s32[]{:S(2)}) async-start(), calls=%async_computation.25 | async-start | bytes 589824 | tf_op jit(solution)/shard_map/reduce_scatter | solution.py:128
  829.2 85.6 %reduce-scatter.24.cloned.1.call-start = ((), (), s32[]{:S(2)}) async-start(), calls=%async_computation.26 | async-start | bytes 589824 | tf_op jit(solution)/shard_map/reduce_scatter | solution.py:128
  834.1 148.8 %reduce-scatter.28.cloned.1.call-start = ((), (), s32[]{:S(2)}) async-start(), calls=%async_computation.28 | async-start | bytes 9437184 | tf_op jit(solution)/shard_map/reduce_scatter | solution.py:128
  848.3 224.8 %reduce-scatter.30.cloned.1.call-start = ((), (), s32[]{:S(2)}) async-start(), calls=%async_computation.29 | async-start | bytes 9437184 | tf_op jit(solution)/shard_map/reduce_scatter | solution.py:128
  862.5 300.7 %reduce-scatter.32.cloned.1.call-start = ((), (), s32[]{:S(2)}) async-start(), calls=%async_computation.30 | async-start | bytes 9437184 | tf_op jit(solution)/shard_map/reduce_scatter | solution.py:128
  877.1 322.8 %reduce-scatter.26.cloned.1.call-start = ((), (), s32[]{:S(2)}) async-start(), calls=%async_computation.27 | async-start | bytes 2359296 | tf_op jit(solution)/shard_map/reduce_scatter | solution.py:128
  883.4 353.3 %reduce-scatter.20.cloned.1.call-start = ((), (), s32[]{:S(2)}) async-start(), calls=%async_computation.24 | async-start | bytes 2359296 | tf_op jit(solution)/shard_map/reduce_scatter | solution.py:128
  891.3 399.7 %reduce-scatter.18.cloned.1.call-start = ((), (), s32[]{:S(2)}) async-start(), calls=%async_computation.23 | async-start | bytes 5242880 | tf_op jit(solution)/shard_map/reduce_scatter | solution.py:128
  898.9 447.7 %reduce-scatter.14.cloned.1.call-start = ((), (), s32[]{:S(2)}) async-start(), calls=%async_computation.19 | async-start | bytes 5242880 | tf_op jit(solution)/shard_map/reduce_scatter | solution.py:128
  985.7 305.3 %copy-start.3 = (bf16[256,2048]{1,0:T(8,128)(2,1)S(1)}, bf16[256,2048]{1,0:T(8,128)(2,1)}, u32[]{:S(2)}) copy-start(bf16[256,2048]{1,0:T(8,128)(2,1)} %param.16) | copy-start | bytes 3145732
  985.7 305.3 %copy-start.31 = (f32[2048]{0:T(1024)S(1)}, f32[2048]{0:T(1024)}, u32[]{:S(2)}) copy-start(f32[2048]{0:T(1024)} %param.17) | copy-start | bytes 24580
  985.7 305.3 %copy-start.38 = (f32[256]{0:T(256)S(1)}, f32[256]{0:T(256)}, u32[]{:S(2)}) copy-start(f32[256]{0:T(256)} %copy-done.37) | copy-start | bytes 3076
  1075.8 270.8 %copy-start.7 = (bf16[256,2048]{1,0:T(8,128)(2,1)S(1)}, bf16[256,2048]{1,0:T(8,128)(2,1)}, u32[]{:S(2)}) copy-start(bf16[256,2048]{1,0:T(8,128)(2,1)} %reduce-scatter.12.cloned.1.call-done) | copy-start | bytes 3145732
  1075.8 270.8 %copy-start.8 = (bf16[256,2048]{1,0:T(8,128)(2,1)S(1)}, bf16[256,2048]{1,0:T(8,128)(2,1)}, u32[]{:S(2)}) copy-start(bf16[256,2048]{1,0:T(8,128)(2,1)} %param.27) | copy-start | bytes 3145732
  1075.8 270.8 %copy-start.30 = (f32[2048]{0:T(1024)S(1)}, f32[2048]{0:T(1024)}, u32[]{:S(2)}) copy-start(f32[2048]{0:T(1024)} %param.22) | copy-start | bytes 24580
  1075.8 270.8 %copy-start.36 = (f32[256]{0:T(256)S(1)}, f32[256]{0:T(256)}, u32[]{:S(2)}) copy-start(f32[256]{0:T(256)} %copy-done.35) | copy-start | bytes 3076
  1075.8 270.8 %copy-start.42 = (f32[256]{0:T(256)S(1)}, f32[256]{0:T(256)}, u32[]{:S(2)}) copy-start(f32[256]{0:T(256)} %copy-done.41) | copy-start | bytes 3076
  1075.9 270.8 %copy-start.44 = (f32[256]{0:T(256)S(1)}, f32[256]{0:T(256)}, u32[]{:S(2)}) copy-start(f32[256]{0:T(256)} %copy-done.43) | copy-start | bytes 3076
  1075.9 270.8 %copy-start.45 = (f32[256]{0:T(256)S(1)}, f32[256]{0:T(256)}, u32[]{:S(2)}) copy-start(f32[256]{0:T(256)} %get-tuple-element.225) | copy-start | bytes 3076
  (46 other events, 1143.9 us)
Sparse Core Ops, SparseCore 0:
  9.6 37.0 all-gather.11
  49.1 52.6 all-gather.9
  103.5 29.1 all-gather.13
  142.7 52.6 reduce-scatter.11
  196.9 82.0 all-gather.17
  281.3 51.0 all-gather.15
  333.9 82.0 all-gather.19
  417.9 51.0 all-gather.23
  470.6 82.0 all-gather.21
  602.9 51.0 reduce-scatter.15
  660.1 52.5 all-gather.25
  829.3 31.2 reduce-scatter.21
  863.5 29.4 reduce-scatter.23
  895.1 87.7 reduce-scatter.27
  985.0 87.9 reduce-scatter.29
  1075.2 87.9 reduce-scatter.31
  1165.3 34.5 reduce-scatter.25
  1202.0 34.6 reduce-scatter.19
  1239.7 51.1 reduce-scatter.17
  1293.7 52.8 reduce-scatter.13
where the time goes:
time: 1370 us; the launch traced here: 1360 us
  waiting for transfers between devices  909 us (66%)
  matrix products  226 us (16%)
  blocking collectives  76.9 us (6%)
  local copies, waits for them, and re-layouts  64.8 us (5%)
  other arithmetic  63.8 us (5%)
  between operations  15.1 us (1%)
    reduce_scatter x11, waiting for transfers between devices, sum_rows(): lax.psum_scatter(partial.astype(jnp.bfloat16), axis, scatter_dimension=0,...  480 us
    all_gather x1, waiting for transfers between devices, per_device(): lax.all_gather(w_down, 'dp', axis=0, tiled=True)  83.7 us
    all_gather x1, waiting for transfers between devices, per_device(): lax.all_gather(w_gate, 'dp', axis=0, tiled=True)  76.9 us
    all_gather x1, waiting for transfers between devices, per_device(): lax.all_gather(w_up, 'dp', axis=0, tiled=True)  69 us
    dot_general x7, matrix products, contract_rows(): lax.dot_general(left_side, right_side, (((0,), (0,)), ((), ())), preferre...  58.9 us
    dot_general x7, matrix products, contract_cols(): lax.dot_general(left_side, right_side, (((1,), (1,)), ((), ())), preferre...  56.7 us
    all_gather x1, waiting for transfers between devices, per_device(): lax.all_gather((residual_own * scale_two_own * mlp_gain[None, :]).astype(...  53.4 us
    all_gather x1, waiting for transfers between devices, per_device(): lax.all_gather(grad_residual_own.astype(jnp.bfloat16), 'tensor', axis=0,...  52.6 us
  transfers between devices with their start and end apart: 20, of which 16 were waited for; matrix products, arithmetic and copies ran while one was open for 13% of the time, Pallas kernels for 0%

commit v1 on v0

--- a/solution.py
+++ b/solution.py
@@ -8,6 +8,27 @@
 EPSILON = 1e-05
 ROPE_BASE = 500000.0
 NEG_LARGE = -1e30
+
+
+def ring_gather(x, axis, dim):
+    devices, place, rows = (lax.axis_size(axis), lax.axis_index(axis), x.shape[dim])
+    forward = [(i, (i + 1) % devices) for i in range(devices)]
+    downward = [(i, (i - 1) % devices) for i in range(devices)]
+    out = jnp.zeros((*x.shape[:dim], devices * rows, *x.shape[dim + 1 :]), x.dtype)
+    out = lax.dynamic_update_slice_in_dim(out, x, place * rows, axis=dim)
+    from_left = from_right = x
+    halfway = devices // 2
+    for step in range(1, halfway + 1):
+        from_left = lax.ppermute(from_left, axis, forward)
+        out = lax.dynamic_update_slice_in_dim(
+            out, from_left, (place - step) % devices * rows, axis=dim
+        )
+        if step < devices - halfway:
+            from_right = lax.ppermute(from_right, axis, downward)
+            out = lax.dynamic_update_slice_in_dim(
+                out, from_right, (place + step) % devices * rows, axis=dim
+            )
+    return out
 
 
 def rotary_tables(length, head_dim):
@@ -149,7 +170,7 @@
         lax.all_gather(w_key, "dp", axis=0, tiled=True),
         lax.all_gather(w_value, "dp", axis=0, tiled=True),
         lax.all_gather(w_out, "dp", axis=0, tiled=True),
-        lax.all_gather(w_gate, "dp", axis=0, tiled=True),
+        ring_gather(w_gate, "dp", 0),
         lax.all_gather(w_up, "dp", axis=0, tiled=True),
         lax.all_gather(w_down, "dp", axis=0, tiled=True),
     )

time: 1370 us -> 1310 us (0.956)
  waiting for transfers between devices: 909 us -> 823 us
  local copies, waits for them, and re-layouts: 64.8 us -> 86.1 us
    all_gather x1 -> x0, waiting for transfers between devices: 76.9 us -> none  [per_device(): lax.all_gather(w_gate, 'dp', axis=0, tiled=True)]
    ppermute x0 -> x7, waiting for transfers between devices: none -> 64.1 us  [the longest x3 64.1 us: ring_gather(): from_right = lax.ppermute(from_right, axis, downward)]
    all_gather x1, waiting for transfers between devices: 38.5 us -> 0.01 us  [per_device(): grad_full = lax.all_gather(cotangent, 'tensor', axis=0, tiled=True)]
    all_gather x1, waiting for transfers between devices: 83.7 us -> 49.5 us  [per_device(): lax.all_gather(w_down, 'dp', axis=0, tiled=True)]
    dynamic_update_slice x0 -> x8, local copies, waits for them, and re-layouts: none -> 14.8 us  [the longest x4 8.09 us: ring_gather(): lax.dynamic_update_slice_in_dim(out, from_left, (place - step) % devices...]
  transfers between devices with their start and end apart: 20 -> 26, of which waited for: 16 -> 17; matrix products, arithmetic and copies ran while one was open for 13% -> 14% of each run, Pallas kernels for 0% -> 0%
where the time goes in v1:
time: 1310 us; the launch traced here: 1300 us
  waiting for transfers between devices  823 us (63%)
  matrix products  222 us (17%)
  local copies, waits for them, and re-layouts  86.1 us (7%)
  blocking collectives  76.9 us (6%)
  other arithmetic  64.5 us (5%)
  between operations  14.8 us (1%)
    reduce_scatter x11, waiting for transfers between devices, sum_rows(): lax.psum_scatter(partial.astype(jnp.bfloat16), axis, scatter_dimension=0,...  481 us
    all_gather x1, waiting for transfers between devices, per_device(): lax.all_gather(w_up, 'dp', axis=0, tiled=True)  69.5 us
    ppermute x3, waiting for transfers between devices, ring_gather(): from_right = lax.ppermute(from_right, axis, downward)  64.1 us
    dot_general x7, matrix products, contract_rows(): lax.dot_general(left_side, right_side, (((0,), (0,)), ((), ())), preferre...  58.8 us
    all_gather x1, waiting for transfers between devices, per_device(): lax.all_gather((residual_own * scale_two_own * mlp_gain[None, :]).astype(...  53.5 us
    dot_general x7, matrix products, contract_cols(): lax.dot_general(left_side, right_side, (((1,), (1,)), ((), ())), preferre...  53.5 us
    all_gather x1, waiting for transfers between devices, per_device(): lax.all_gather(grad_residual_own.astype(jnp.bfloat16), 'tensor', axis=0,...  52.6 us
    all_gather x1, waiting for transfers between devices, per_device(): lax.all_gather((input_own * scale_one * attn_gain[None, :]).astype(jnp.bf...  50.3 us
  transfers between devices with their start and end apart: 26, of which 17 were waited for; matrix products, arithmetic and copies ran while one was open for 14% of the time, Pallas kernels for 0%

profile of v1, /device:TPU:0, one launch (start us, length us, event | category | flops | bytes accessed | tf_op | source)
XLA Modules:
  0.0 1300.5 jit_solution(10064902112232264345)
XLA Ops:
  14.4 18.8 %all_gather.32 = bf16[2048,128]{1,0:T(8,128)(2,1)S(1)} all-gather(bf16[256,128]{1,0:T(8,128)(2,1)S(1)} %copy-done.29), channel_id=1, replica_groups=mesh['dp'=8,'tensor'=4] {'dp'}, dimensions={0}, use_global_device_ids=true | all-gather | bytes 589824 | tf_op jit(solution)/shard_map/all_gather | solution.py:170
  33.2 18.3 %all_gather.31 = bf16[2048,128]{1,0:T(8,128)(2,1)} all-gather(bf16[256,128]{1,0:T(8,128)(2,1)S(1)} %copy-done.30), channel_id=1, replica_groups=mesh['dp'=8,'tensor'=4] {'dp'}, dimensions={0}, use_global_device_ids=true | all-gather | bytes 589824 | tf_op jit(solution)/shard_map/all_gather | solution.py:171
  51.5 50.3 %all-gather.9.cloned.1.call-done = bf16[1024,2048]{1,0:T(8,128)(2,1)} async-done(((bf16[256,2048]{1,0:T(8,128)(2,1)}), bf16[1024,2048]{1,0:T(8,128)(2,1)}) %all-gather.9.cloned.1.call-update) | async-done | bytes 4194320 | tf_op jit(solution)/shard_map/all_gather | solution.py:185
  123.2 14.8 %while.26 = (s32[]{:T(128)}, bf16[2,512,512]{2,1,0:T(8,128)(2,1)}, f32[2,2,4,512,1]{3,2,1,4,0:T(4,128)S(1)}, bf16[2,512,2,64]{1,3,2,0:T(8,128)(2,1)S(1)}, s32[2,...) while((s32[]{:T(128)}, bf16[2,512,512]{2,1,0:T(8,128)(2,1)}, ...), condition=%wide.region_4.5_spmd, body=%wide.region_1.4_spmd.sunk | while | flops 564130816 | bytes 32913000 | solution.py:205
  146.4 50.8 %reduce-scatter.12.cloned.1.call-done = bf16[256,2048]{1,0:T(8,128)(2,1)} async-done(((bf16[1024,2048]{1,0:T(8,128)(2,1)}), bf16[256,2048]{1,0:T(8,128)(2,1)}) %reduce-scatter.12.cloned.1.call-update) | async-done | bytes 1048592 | tf_op jit(solution)/shard_map/reduce_scatter | solution.py:149
  204.2 22.2 %collective-permute-done.1 = bf16[256,2048]{1,0:T(8,128)(2,1)} collective-permute-done((bf16[256,2048]{1,0:T(8,128)(2,1)}, bf16[256,2048]{1,0:T(8,128)(2,1)}, u32[]{:S(2)}, u32[]{:S(2)}) %collective-permute-start.1) | collective-permute-done | bytes 1048608 | tf_op jit(solution)/shard_map/ppermute | solution.py:27
  235.5 15.0 %collective-permute-done.3 = bf16[256,2048]{1,0:T(8,128)(2,1)} collective-permute-done((bf16[256,2048]{1,0:T(8,128)(2,1)}, bf16[256,2048]{1,0:T(8,128)(2,1)}, u32[]{:S(2)}, u32[]{:S(2)}) %collective-permute-start.3) | collective-permute-done | bytes 1048608 | tf_op jit(solution)/shard_map/ppermute | solution.py:27
  266.0 26.9 %collective-permute-done.5 = bf16[256,2048]{1,0:T(8,128)(2,1)S(1)} collective-permute-done((bf16[256,2048]{1,0:T(8,128)(2,1)}, bf16[256,2048]{1,0:T(8,128)(2,1)S(1)}, u32[]{:S(2)}, u32[]{:S(2)}) %collective-permute-start.5) | collective-permute-done | bytes 1048608 | tf_op jit(solution)/shard_map/ppermute | solution.py:27
  295.0 49.5 %all-gather.19.cloned.1.call-done = bf16[2048,2048]{1,0:T(8,128)(2,1)} async-done(((bf16[256,2048]{1,0:T(8,128)(2,1)}), bf16[2048,2048]{1,0:T(8,128)(2,1)}) %all-gather.19.cloned.1.call-update) | async-done | bytes 8388624 | tf_op jit(solution)/shard_map/all_gather | solution.py:175
  344.5 14.7 %fusion.76 = f32[1024,2048]{1,0:T(8,128)} fusion(bf16[1024,2048]{1,0:T(8,128)(2,1)} %all-gather.21.cloned.1.call-done, bf16[2048,2048]{1,0:T(8,128)(2,1)} %all-gather.19.cloned.1.call-done), kind=kOutput, calls=%fused_computation.152 | convolution fusion | flops 8589934592 | bytes 20971520 | tf_op jit(solution)/shard_map/dot_general | solution.py:224
  359.2 69.5 %all-gather.17.cloned.1.call-done = bf16[2048,2048]{1,0:T(8,128)(2,1)} async-done(((bf16[256,2048]{1,0:T(8,128)(2,1)}), bf16[2048,2048]{1,0:T(8,128)(2,1)}) %all-gather.17.cloned.1.call-update) | async-done | bytes 8388624 | tf_op jit(solution)/shard_map/all_gather | solution.py:174
  428.7 53.5 %all-gather.15.cloned.1.call-done = bf16[1024,2048]{1,0:T(8,128)(2,1)} async-done(((bf16[256,2048]{1,0:T(8,128)(2,1)}), bf16[1024,2048]{1,0:T(8,128)(2,1)}) %all-gather.15.cloned.1.call-update) | async-done | bytes 4194320 | tf_op jit(solution)/shard_map/all_gather | solution.py:209
  482.2 15.5 %fusion.75 = f32[1024,2048]{1,0:T(8,128)} fusion(bf16[1024,2048]{1,0:T(8,128)(2,1)} %all-gather.15.cloned.1.call-done, bf16[2048,2048]{1,0:T(8,128)(2,1)} %all-gather.17.cloned.1.call-done), kind=kOutput, calls=%fused_computation.151 | convolution fusion | flops 8589934592 | bytes 20971520 | tf_op jit(solution)/shard_map/dot_general | solution.py:216
  497.8 19.7 %multiply_convert_fusion.2 = (bf16[1024,2048]{1,0:T(8,128)(2,1)}, bf16[1024,2048]{1,0:T(8,128)(2,1)}, bf16[1024,2048]{1,0:T(8,128)(2,1)}) fusion(f32[1024,2048]{1,0:T(8,128)} %fusion.76, f32[1024,2048]{1,0:T(8,128)} %fusion.75, bf16[1024,2048]{1,0:T(8,128)(2,1)S(1)} %copy-done.43, bf16[2048,2048]{1,0:T(8,128)(2,1)} %constant_dynamic-update-slice_fusion.1), kind=kOutput, calls=%fused_computation.65 | convolution fusion | flops 8621391872 | bytes 41943040 | tf_op jit(solution)/shard_map/dot_general | solution.py:215
  517.4 13.2 %fusion.77 = f32[1024,2048]{1,0:T(8,128)S(1)} fusion(bf16[1024,2048]{1,0:T(8,128)(2,1)} %get-tuple-element.211, bf16[2048,2048]{1,0:T(8,128)(2,1)} %all-gather.17.cloned.1.call-done), kind=kOutput, calls=%fused_computation.153 | convolution fusion | flops 8589934592 | bytes 20971520 | tf_op jit(solution)/shard_map/dot_general | solution.py:88
  543.6 52.7 %reduce-scatter.16.cloned.1.call-done = bf16[256,2048]{1,0:T(8,128)(2,1)} async-done(((bf16[1024,2048]{1,0:T(8,128)(2,1)}), bf16[256,2048]{1,0:T(8,128)(2,1)}) %reduce-scatter.16.cloned.1.call-update) | async-done | bytes 1048592 | tf_op jit(solution)/shard_map/reduce_scatter | solution.py:149
  602.9 52.6 %all-gather.23.cloned.1.call-done = bf16[1024,2048]{1,0:T(8,128)(2,1)} async-done(((bf16[256,2048]{1,0:T(8,128)(2,1)}), bf16[1024,2048]{1,0:T(8,128)(2,1)}) %all-gather.23.cloned.1.call-update) | async-done | bytes 4194320 | tf_op jit(solution)/shard_map/all_gather | solution.py:239
  661.7 104.8 %while.27 = (s32[]{:T(128)}, f32[2,512,8,64]{1,0,3,2:T(2,128)}, f32[2,512,2,64]{1,0,3,2:T(2,128)}, bf16[2,512,2,64]{1,3,2,0:T(8,128)(2,1)}, bf16[2,512,2,64]{1,3...) while((s32[]{:T(128)}, f32[2,512,8,64]{1,0,3,2:T(2,128)}, ...), condition=%wide.region_12.13_spmd, body=%wide.region_10.12_spmd.sunk | while | flops 1365045760 | bytes 140994448 | solution.py:247
  682.6 19.7 %dynamic_update_slice.70 = f32[2,512,8,64]{1,0,3,2:T(2,128)} dynamic-update-slice(f32[2,512,8,64]{1,0,3,2:T(2,128)} %get-tuple-element.382, f32[1,512,8,64]{1,0,3,2:T(1,128)S(1)} %copy.94, s32[]{:T(128)} %get-tuple-element.381, s32[]{:T(128)} %constant.118.clone.1..sunk, s32[]{:T(128)} %constant.118.clone.1..sunk, s32[]{:T(128)} %constant.118.clone.1..sunk) | dynamic-update-slice | bytes 2097156 | tf_op jit(solution)/shard_map/while/body/jit(dynamic_update_index_in_dim)/dynamic_update_slice | solution.py:247
  734.9 19.7 %dynamic_update_slice.70 = f32[2,512,8,64]{1,0,3,2:T(2,128)} dynamic-update-slice(f32[2,512,8,64]{1,0,3,2:T(2,128)} %get-tuple-element.382, f32[1,512,8,64]{1,0,3,2:T(1,128)S(1)} %copy.94, s32[]{:T(128)} %get-tuple-element.381, s32[]{:T(128)} %constant.118.clone.1..sunk, s32[]{:T(128)} %constant.118.clone.1..sunk, s32[]{:T(128)} %constant.118.clone.1..sunk) | dynamic-update-slice | bytes 2097156 | tf_op jit(solution)/shard_map/while/body/jit(dynamic_update_index_in_dim)/dynamic_update_slice | solution.py:247
  776.9 14.1 %convolution_convert_fusion.1 = bf16[2048,2048]{1,0:T(8,128)(2,1)} fusion(bf16[1024,2048]{1,0:T(8,128)(2,1)} %all-gather.15.cloned.1.call-done, bf16[1024,2048]{1,0:T(8,128)(2,1)} %get-tuple-element.210), kind=kOutput, calls=%fused_computation.70 | convolution fusion | flops 8594128896 | bytes 16777216 | tf_op jit(solution)/shard_map/dot_general | solution.py:82
  791.1 14.1 %convolution_convert_fusion = bf16[2048,2048]{1,0:T(8,128)(2,1)} fusion(bf16[1024,2048]{1,0:T(8,128)(2,1)} %all-gather.15.cloned.1.call-done, bf16[1024,2048]{1,0:T(8,128)(2,1)} %get-tuple-element.211), kind=kOutput, calls=%fused_computation.69 | convolution fusion | flops 8594128896 | bytes 16777216 | tf_op jit(solution)/shard_map/dot_general | solution.py:82
  805.6 14.0 %convert_bitcast_fusion = bf16[2048,2048]{0,1:T(8,128)(2,1)} fusion(bf16[1024,2048]{1,0:T(8,128)(2,1)} %get-tuple-element.212, bf16[1024,2048]{1,0:T(8,128)(2,1)} %all-gather.21.cloned.1.call-done), kind=kOutput, calls=%fused_computation.61 | convolution fusion | flops 8594128896 | bytes 16777216 | tf_op jit(solution)/shard_map/dot_general | solution.py:82
  841.5 14.3 %convolution_convert_fusion.2 = bf16[1024,2048]{1,0:T(8,128)(2,1)} fusion(bf16[1024,2048]{1,0:T(8,128)(2,1)} %get-tuple-element.212, bf16[2048,2048]{1,0:T(8,128)(2,1)} %all-gather.19.cloned.1.call-done), kind=kOutput, calls=%fused_computation.77 | convolution fusion | flops 8592031744 | bytes 16777216 | tf_op jit(solution)/shard_map/dot_general | solution.py:88
  858.8 66.7 %reduce-scatter.28.cloned.1.call-done = bf16[256,2048]{1,0:T(8,128)(2,1)} async-done(((bf16[2048,2048]{1,0:T(8,128)(2,1)}), bf16[256,2048]{1,0:T(8,128)(2,1)}) %reduce-scatter.28.cloned.1.call-update) | async-done | bytes 1048592 | tf_op jit(solution)/shard_map/reduce_scatter | solution.py:149
  928.3 87.4 %reduce-scatter.30.cloned.1.call-done = bf16[256,2048]{1,0:T(8,128)(2,1)} async-done(((bf16[2048,2048]{1,0:T(8,128)(2,1)}), bf16[256,2048]{1,0:T(8,128)(2,1)}) %reduce-scatter.30.cloned.1.call-update) | async-done | bytes 1048592 | tf_op jit(solution)/shard_map/reduce_scatter | solution.py:149
  1018.5 87.3 %reduce-scatter.32.cloned.1.call-done = bf16[256,2048]{0,1:T(8,128)(2,1)} async-done(((bf16[2048,2048]{0,1:T(8,128)(2,1)}), bf16[256,2048]{0,1:T(8,128)(2,1)}) %reduce-scatter.32.cloned.1.call-update) | async-done | bytes 1048592 | tf_op jit(solution)/shard_map/reduce_scatter | solution.py:149
  1108.4 34.2 %reduce-scatter.26.cloned.1.call-done = bf16[256,512]{1,0:T(8,128)(2,1)} async-done(((bf16[2048,512]{1,0:T(8,128)(2,1)}), bf16[256,512]{1,0:T(8,128)(2,1)}) %reduce-scatter.26.cloned.1.call-update) | async-done | bytes 262160 | tf_op jit(solution)/shard_map/reduce_scatter | solution.py:149
  1144.4 35.0 %reduce-scatter.20.cloned.1.call-done = bf16[256,512]{1,0:T(8,128)(2,1)} async-done(((bf16[2048,512]{1,0:T(8,128)(2,1)}), bf16[256,512]{1,0:T(8,128)(2,1)}) %reduce-scatter.20.cloned.1.call-update) | async-done | bytes 262160 | tf_op jit(solution)/shard_map/reduce_scatter | solution.py:149
  1181.2 52.3 %reduce-scatter.18.cloned.1.call-done = bf16[256,2048]{1,0:T(8,128)(2,1)} async-done(((bf16[1024,2048]{1,0:T(8,128)(2,1)}), bf16[256,2048]{1,0:T(8,128)(2,1)}) %reduce-scatter.18.cloned.1.call-update) | async-done | bytes 1048592 | tf_op jit(solution)/shard_map/reduce_scatter | solution.py:149
  1235.4 39.8 %all-reduce = (f32[2048]{0:T(1024)}, f32[2048]{0:T(1024)}) all-reduce(f32[2048]{0:T(1024)S(1)} %get-tuple-element.166, f32[2048]{0:T(1024)S(1)} %copy-done.31), channel_id=1, replica_groups=mesh['dp'=8,'tensor'=4] {'dp','tensor'}, use_global_device_ids=true, to_apply=%region_23.24 | all-reduce | flops 4096 | bytes 32768 | tf_op jit(solution)/shard_map/psum | solution.py:283
  1275.2 14.2 %reduce-scatter.14.cloned.1.call-done = bf16[256,2048]{1,0:T(8,128)(2,1)} async-done(((bf16[1024,2048]{1,0:T(8,128)(2,1)}), bf16[256,2048]{1,0:T(8,128)(2,1)}) %reduce-scatter.14.cloned.1.call-update) | async-done | bytes 1048592 | tf_op jit(solution)/shard_map/reduce_scatter | solution.py:149
  (287 shorter events, 229.1 us)
Async XLA Ops:
  7.2 44.3 %all-gather.11.cloned.1.call-start = ((), (), s32[]{:S(2)}) async-start(), calls=%async_computation.12 | async-start | bytes 2359296 | tf_op jit(solution)/shard_map/all_gather | solution.py:169
  7.9 93.9 %all-gather.9.cloned.1.call-start = ((), (), s32[]{:S(2)}) async-start(), calls=%async_computation.11 | async-start | bytes 5242880 | tf_op jit(solution)/shard_map/all_gather | solution.py:185
  13.2 124.8 %all-gather.13.cloned.1.call-start = ((), (), s32[]{:S(2)}) async-start(), calls=%async_computation.13 | async-start | bytes 2359296 | tf_op jit(solution)/shard_map/all_gather | solution.py:172
  13.9 183.3 %reduce-scatter.12.cloned.1.call-start = ((), (), s32[]{:S(2)}) async-start(), calls=%async_computation.14 | async-start | bytes 5242880 | tf_op jit(solution)/shard_map/reduce_scatter | solution.py:149
  144.3 150.7 %all-gather.21.cloned.1.call-start = ((), (), s32[]{:S(2)}) async-start(), calls=%async_computation.19 | async-start | bytes 5242880 | tf_op jit(solution)/shard_map/all_gather | solution.py:223
  144.9 199.6 %all-gather.19.cloned.1.call-start = ((), (), s32[]{:S(2)}) async-start(), calls=%async_computation.17 | async-start | bytes 9437184 | tf_op jit(solution)/shard_map/all_gather | solution.py:175
  145.5 283.2 %all-gather.17.cloned.1.call-start = ((), (), s32[]{:S(2)}) async-start(), calls=%async_computation.16 | async-start | bytes 9437184 | tf_op jit(solution)/shard_map/all_gather | solution.py:174
  146.3 336.0 %all-gather.15.cloned.1.call-start = ((), (), s32[]{:S(2)}) async-start(), calls=%async_computation.15 | async-start | bytes 5242880 | tf_op jit(solution)/shard_map/all_gather | solution.py:209
  146.3 57.9 %collective-permute-start = (bf16[256,2048]{1,0:T(8,128)(2,1)}, bf16[256,2048]{1,0:T(8,128)(2,1)}, u32[]{:S(2)}, u32[]{:S(2)}) collective-permute-start(bf16[256,2048]{1,0:T(8,128)(2,1)} %param.23), channel_id=1, source_target_pairs={{0,4},{4,8},{8,12},{12,16},{16,20},{20,24},{24,28},{28,0},{1,5},{5... | collective-permute-start | bytes 3145736 | tf_op jit(solution)/shard_map/ppermute | solution.py:22
  198.9 400.3 %copy-start.32 = (f32[256]{0:T(256)}, f32[256]{0:T(256)S(1)}, u32[]{:S(2)}) copy-start(f32[256]{0:T(256)S(1)} %get-tuple-element.228) | copy-start | bytes 3076
  198.9 400.3 %copy-start.38 = (f32[256]{0:T(256)}, f32[256]{0:T(256)S(1)}, u32[]{:S(2)}) copy-start(f32[256]{0:T(256)S(1)} %get-tuple-element.227) | copy-start | bytes 3076
  201.5 394.8 %reduce-scatter.16.cloned.1.call-start = ((), (), s32[]{:S(2)}) async-start(), calls=%async_computation.20 | async-start | bytes 5242880 | tf_op jit(solution)/shard_map/reduce_scatter | solution.py:149
  201.5 24.9 %collective-permute-start.1 = (bf16[256,2048]{1,0:T(8,128)(2,1)}, bf16[256,2048]{1,0:T(8,128)(2,1)}, u32[]{:S(2)}, u32[]{:S(2)}) collective-permute-start(bf16[256,2048]{1,0:T(8,128)(2,1)} %param.23), channel_id=1, source_target_pairs={{0,28},{4,0},{8,4},{12,8},{16,12},{20,16},{24,20},{28,24},{1,29},{... | collective-permute-start | bytes 3145736 | tf_op jit(solution)/shard_map/ppermute | solution.py:27
  204.2 26.0 %collective-permute-start.2 = (bf16[256,2048]{1,0:T(8,128)(2,1)}, bf16[256,2048]{1,0:T(8,128)(2,1)}, u32[]{:S(2)}, u32[]{:S(2)}) collective-permute-start(bf16[256,2048]{1,0:T(8,128)(2,1)} %collective-permute-done), channel_id=1, source_target_pairs={{0,4},{4,8},{8,12},{12,16},{16,20},{20,24},{24,28},{28,0},{1,5},{5... | collective-permute-start | bytes 3145736 | tf_op jit(solution)/shard_map/ppermute | solution.py:22
  226.4 24.1 %collective-permute-start.3 = (bf16[256,2048]{1,0:T(8,128)(2,1)}, bf16[256,2048]{1,0:T(8,128)(2,1)}, u32[]{:S(2)}, u32[]{:S(2)}) collective-permute-start(bf16[256,2048]{1,0:T(8,128)(2,1)} %collective-permute-done.1), channel_id=1, source_target_pairs={{0,28},{4,0},{8,4},{12,8},{16,12},{20,16},{24,20},{28,24},{1,29},{... | collective-permute-start | bytes 3145736 | tf_op jit(solution)/shard_map/ppermute | solution.py:27
  230.2 26.4 %collective-permute-start.4 = (bf16[256,2048]{1,0:T(8,128)(2,1)}, bf16[256,2048]{1,0:T(8,128)(2,1)}, u32[]{:S(2)}, u32[]{:S(2)}) collective-permute-start(bf16[256,2048]{1,0:T(8,128)(2,1)} %collective-permute-done.2), channel_id=1, source_target_pairs={{0,4},{4,8},{8,12},{12,16},{16,20},{20,24},{24,28},{28,0},{1,5},{5... | collective-permute-start | bytes 3145736 | tf_op jit(solution)/shard_map/ppermute | solution.py:22
  250.6 42.3 %collective-permute-start.5 = (bf16[256,2048]{1,0:T(8,128)(2,1)}, bf16[256,2048]{1,0:T(8,128)(2,1)S(1)}, u32[]{:S(2)}, u32[]{:S(2)}) collective-permute-start(bf16[256,2048]{1,0:T(8,128)(2,1)} %collective-permute-done.3), channel_id=1, source_target_pairs={{0,28},{4,0},{8,4},{12,8},{16,12},{20,16},{24,20},{28,24},{1,29},{... | collective-permute-start | bytes 3145736 | tf_op jit(solution)/shard_map/ppermute | solution.py:27
  256.6 37.3 %collective-permute-start.6 = (bf16[256,2048]{1,0:T(8,128)(2,1)}, bf16[256,2048]{1,0:T(8,128)(2,1)S(1)}, u32[]{:S(2)}, u32[]{:S(2)}) collective-permute-start(bf16[256,2048]{1,0:T(8,128)(2,1)} %collective-permute-done.4), channel_id=1, source_target_pairs={{0,4},{4,8},{8,12},{12,16},{16,20},{20,24},{24,28},{28,0},{1,5},{5... | collective-permute-start | bytes 3145736 | tf_op jit(solution)/shard_map/ppermute | solution.py:22
  543.5 112.1 %all-gather.23.cloned.1.call-start = ((), (), s32[]{:S(2)}) async-start(), calls=%async_computation.21 | async-start | bytes 5242880 | tf_op jit(solution)/shard_map/all_gather | solution.py:239
  602.8 253.0 %reduce-scatter.22.cloned.1.call-start = ((), (), s32[]{:S(2)}) async-start(), calls=%async_computation.24 | async-start | bytes 589824 | tf_op jit(solution)/shard_map/reduce_scatter | solution.py:149
  772.0 85.4 %reduce-scatter.24.cloned.1.call-start = ((), (), s32[]{:S(2)}) async-start(), calls=%async_computation.25 | async-start | bytes 589824 | tf_op jit(solution)/shard_map/reduce_scatter | solution.py:149
  776.9 148.6 %reduce-scatter.28.cloned.1.call-start = ((), (), s32[]{:S(2)}) async-start(), calls=%async_computation.27 | async-start | bytes 9437184 | tf_op jit(solution)/shard_map/reduce_scatter | solution.py:149
  791.0 224.7 %reduce-scatter.30.cloned.1.call-start = ((), (), s32[]{:S(2)}) async-start(), calls=%async_computation.28 | async-start | bytes 9437184 | tf_op jit(solution)/shard_map/reduce_scatter | solution.py:149
  805.2 300.7 %reduce-scatter.32.cloned.1.call-start = ((), (), s32[]{:S(2)}) async-start(), calls=%async_computation.29 | async-start | bytes 9437184 | tf_op jit(solution)/shard_map/reduce_scatter | solution.py:149
  819.7 322.9 %reduce-scatter.26.cloned.1.call-start = ((), (), s32[]{:S(2)}) async-start(), calls=%async_computation.26 | async-start | bytes 2359296 | tf_op jit(solution)/shard_map/reduce_scatter | solution.py:149
  826.1 353.2 %reduce-scatter.20.cloned.1.call-start = ((), (), s32[]{:S(2)}) async-start(), calls=%async_computation.23 | async-start | bytes 2359296 | tf_op jit(solution)/shard_map/reduce_scatter | solution.py:149
  833.9 399.6 %reduce-scatter.18.cloned.1.call-start = ((), (), s32[]{:S(2)}) async-start(), calls=%async_computation.22 | async-start | bytes 5242880 | tf_op jit(solution)/shard_map/reduce_scatter | solution.py:149
  841.5 447.9 %reduce-scatter.14.cloned.1.call-start = ((), (), s32[]{:S(2)}) async-start(), calls=%async_computation.18 | async-start | bytes 5242880 | tf_op jit(solution)/shard_map/reduce_scatter | solution.py:149
  928.3 305.2 %copy-start.3 = (bf16[256,2048]{1,0:T(8,128)(2,1)S(1)}, bf16[256,2048]{1,0:T(8,128)(2,1)}, u32[]{:S(2)}) copy-start(bf16[256,2048]{1,0:T(8,128)(2,1)} %param.16) | copy-start | bytes 3145732
  928.3 305.2 %copy-start.28 = (f32[2048]{0:T(1024)S(1)}, f32[2048]{0:T(1024)}, u32[]{:S(2)}) copy-start(f32[2048]{0:T(1024)} %param.17) | copy-start | bytes 24580
  928.3 305.2 %copy-start.35 = (f32[256]{0:T(256)S(1)}, f32[256]{0:T(256)}, u32[]{:S(2)}) copy-start(f32[256]{0:T(256)} %copy-done.34) | copy-start | bytes 3076
  1018.5 270.9 %copy-start.27 = (f32[2048]{0:T(1024)S(1)}, f32[2048]{0:T(1024)}, u32[]{:S(2)}) copy-start(f32[2048]{0:T(1024)} %param.22) | copy-start | bytes 24580
  (48 other events, 2718.2 us)
Sparse Core Ops, SparseCore 0:
  9.6 37.0 all-gather.10
  49.1 52.6 all-gather.8
  103.4 29.1 all-gather.12
  144.5 52.6 reduce-scatter.11
  198.9 52.5 all-gather.20
  252.9 91.5 all-gather.18
  346.1 82.5 all-gather.16
  431.2 51.0 all-gather.14
  543.6 52.5 reduce-scatter.15
  603.0 52.5 all-gather.22
  772.1 31.2 reduce-scatter.21
  806.1 29.4 reduce-scatter.23
  837.9 87.6 reduce-scatter.27
  927.7 87.9 reduce-scatter.29
  1017.8 87.9 reduce-scatter.31
  1108.0 34.5 reduce-scatter.25
  1144.7 34.6 reduce-scatter.19
  1182.2 51.2 reduce-scatter.17
  1236.5 52.8 reduce-scatter.13
